TPU v7x, 32 devices: a whole 2x2x4 slice. The times are simulated.
32 devices in a mesh: groups: 2 (over y), seq: 4 (over z), fsdp: 2 (over x), sub: 2 (over core).
Axes of the slice: x: 2, y: 2, z: 4, core: 2. Of those that a mesh axis runs over, the one named last changes fastest.
Arguments:
- tokens: bfloat16 [2048, 8192], P(('groups', 'seq')), parts along dimension 0, may hold values from -400 to 400
- norm_gain: float32 [8192], replicated, may hold values from 0.1 to 1.9
- w_query: bfloat16 [8, 16, 8192], P(('seq', 'sub'), 'fsdp'), may hold values from -0.0625 to 0.0625
- w_key: bfloat16 [8, 16, 8192], P(('seq', 'sub'), 'fsdp'), may hold values from -0.0625 to 0.0625
- w_value: bfloat16 [8, 128, 8192], P(('seq', 'sub'), 'fsdp'), may hold values from -5 to 5
- head_gain: float32 [128], replicated, may hold values from 0.1 to 1.9
- w_out: bfloat16 [8, 128, 8192], P('seq', None, ('fsdp', 'sub')), may hold values from -0.1875 to 0.1875
Outputs:
- mixed: bfloat16 [2048, 8192], P(('groups', 'seq'), ('fsdp', 'sub')), parts along dimension 0
There are 2 independent parts, one for each index of `groups`. A program takes and returns all parts, laid end to end along the dimension named above; an argument that names none is the same for every part. Nothing has to cross between parts.
All inputs are finite; a program needn't handle non-finite values.
Results may differ from a plain program's by a relative error of at most 0.0084.
Values may be sent and summed in bfloat16 or wider, within the bound.
No kernel may reach another device: no remote copies, remote signals or barrier semaphores. Data moves between devices by JAX's collectives and lax.ppermute only.
A program may use at most 64 MiB of HBM per device.

v0:
```python
import math
import jax
import jax.numpy as jnp
import numpy as np
from jax import lax
from jax.sharding import PartitionSpec as P

BLOCK = 512


def taylor_first(vectors):
    feature_count = vectors.shape[0]
    first_row, second_row = np.triu_indices(feature_count, 1)
    cross_terms = vectors[first_row] * vectors[second_row] / 4.0
    squares = vectors * vectors / (4.0 * math.sqrt(2.0))
    leading = jnp.ones((1,) + vectors.shape[1:], jnp.float32)
    return jnp.concatenate([leading, vectors / 2.0, cross_terms, squares], 0)


def head_norm(numerator, head_gain, channel_axis):
    widened = numerator.astype(jnp.float32)
    meansq = jnp.mean(widened * widened, axis=channel_axis, keepdims=True)
    gain_shape = tuple((-1 if axis_pos == channel_axis else 1 for axis_pos in range(widened.ndim)))
    return (widened * lax.rsqrt(meansq + 1e-06) * head_gain.reshape(gain_shape)).astype(
        jnp.bfloat16
    )


def attend(queries, key_vectors, values_local):
    length = queries.shape[1]
    nblocks = length // BLOCK
    channels = values_local.shape[0]
    query_feats = taylor_first(queries.astype(jnp.float32)).astype(jnp.bfloat16)
    key_feats = taylor_first(key_vectors.astype(jnp.float32)).astype(jnp.bfloat16)
    taylor_width = query_feats.shape[0]
    contrib = jnp.einsum(
        "fbj,ebj->bfe",
        key_feats.reshape(taylor_width, nblocks, BLOCK),
        values_local.reshape(channels, nblocks, BLOCK),
        preferred_element_type=jnp.float32,
    )
    prefix = jnp.concatenate([jnp.zeros_like(contrib[:1]), jnp.cumsum(contrib[:-1], axis=0)], 0)
    prior_state = prefix.astype(jnp.bfloat16)
    carried = jnp.einsum(
        "bfe,fbt->bet",
        prior_state,
        query_feats.reshape(taylor_width, nblocks, BLOCK),
        preferred_element_type=jnp.float32,
    )
    earlier = lax.broadcasted_iota(jnp.int32, (BLOCK, BLOCK), 0)
    column_pos = lax.broadcasted_iota(jnp.int32, (BLOCK, BLOCK), 1)
    causal = earlier <= column_pos

    def one_block(block_index):
        offset = block_index * BLOCK
        query_block = lax.dynamic_slice_in_dim(queries, offset, BLOCK, 1)
        key_block = lax.dynamic_slice_in_dim(key_vectors, offset, BLOCK, 1)
        value_block = lax.dynamic_slice_in_dim(values_local, offset, BLOCK, 1)
        scores = jnp.einsum("fj,ft->jt", key_block, query_block, preferred_element_type=jnp.float32)
        kernel = 1.0 + scores / 4.0 + scores * scores / 32.0
        weight = jnp.where(causal, kernel, 0.0).astype(jnp.bfloat16)
        return jnp.einsum("ej,jt->et", value_block, weight, preferred_element_type=jnp.float32)

    local_part = lax.map(one_block, jnp.arange(nblocks, dtype=jnp.int32))
    numerator = (local_part + carried).astype(jnp.bfloat16)
    return jnp.transpose(numerator, (1, 0, 2)).reshape(channels, length)


def per_device(tokens, norm_gain, w_query, w_key, w_value, head_gain, w_out):
    feat_dev = w_query.shape[1]
    inputs = tokens.astype(jnp.float32)
    meansq = jnp.mean(inputs * inputs, axis=1, keepdims=True)
    normed = (inputs * lax.rsqrt(meansq + 1e-05) * norm_gain).astype(jnp.bfloat16)
    stacked = jnp.concatenate([w_query, w_key, w_value], 1)
    head_weights, out_weights = (
        lax.all_gather(stacked, "seq", axis=0, tiled=True),
        lax.all_gather(w_out, "seq", axis=0, tiled=True),
    )
    projected = jnp.einsum(
        "hcd,td->hct", head_weights, normed, preferred_element_type=jnp.float32
    ).astype(jnp.bfloat16)
    by_head = lax.all_to_all(projected, "seq", split_axis=0, concat_axis=2, tiled=True)
    qk_local = by_head[:, : 2 * feat_dev]
    values_local = by_head[0, 2 * feat_dev :]
    qk_whole = lax.all_gather(qk_local, "fsdp", axis=0, tiled=True)
    length = qk_whole.shape[2]
    queries = qk_whole[:, :feat_dev].reshape(-1, length)
    key_vectors = qk_whole[:, feat_dev:].reshape(-1, length)
    numerator = attend(queries, key_vectors, values_local)
    heads_total = out_weights.shape[0]
    head_width = out_weights.shape[1]
    by_token = lax.all_to_all(numerator[None], "seq", split_axis=2, concat_axis=0, tiled=True)
    everyone = lax.all_gather(by_token[None], ("fsdp", "sub"), axis=0, tiled=True)
    arranged = everyone.reshape(
        lax.axis_size("fsdp"),
        lax.axis_size("sub"),
        everyone.shape[1],
        everyone.shape[2],
        everyone.shape[3],
    )
    arranged = jnp.transpose(arranged, (2, 1, 0, 3, 4)).reshape(heads_total, head_width, -1)
    attended = head_norm(arranged, head_gain, 1)
    mixed = jnp.einsum("het,hed->td", attended, out_weights, preferred_element_type=jnp.float32)
    return mixed.astype(jnp.bfloat16)


def solution(mesh):
    in_specs = (
        P(("groups", "seq"), None),
        P(),
        P(("seq", "sub"), "fsdp", None),
        P(("seq", "sub"), "fsdp", None),
        P(("seq", "sub"), "fsdp", None),
        P(),
        P("seq", None, ("fsdp", "sub")),
    )
    out_specs = P(("groups", "seq"), ("fsdp", "sub"))
    return jax.shard_map(
        per_device, mesh=mesh, in_specs=in_specs, out_specs=out_specs, check_vma=False
    )
```

profile of v0, /device:TPU:0, one launch (start us, length us, event | category | flops | bytes accessed | tf_op | source)
XLA Modules:
  0.0 208.2 jit_solution(16304550115294808762)
XLA Ops:
  6.5 0.0 copy-start.2
  6.5 0.0 all-gather.4.cloned.1.call-start
  6.5 2.5 %pad_maximum_fusion = bf16[1,80,8192]{2,1,0:T(8,128)(2,1)} fusion(bf16[1,64,8192]{2,1,0:T(8,128)(2,1)} %param.21, bf16[1,8,8192]{2,1,0:T(8,128)(2,1)} %param.20, bf16[1,8,8192]{2,1,0:T(8,128)(2,1)} %param.19), kind=kLoop, calls=%fused_computation.32 | loop fusion | flops 3932160 | bytes 2621440 | tf_op jit(solution)/shard_map/concatenate | solution.py:74
  9.0 0.0 all-gather.4.cloned.1.call-update
  9.0 0.0 all-gather.6.cloned.1.call-start
  9.1 0.7 all-gather.6.cloned.1.call-update
  9.8 3.1 %fusion.18 = f32[256]{0:T(256)S(1)} fusion(bf16[256,8192]{1,0:T(8,128)(2,1)} %param.17), kind=kLoop, calls=%fused_computation.23 | loop fusion | flops 6291200 | bytes 4195328 | tf_op jit(solution)/shard_map/reduce_sum | solution.py:72
  12.9 0.0 copy-start.1
  12.9 0.0 copy-start
  12.9 97.0 %all-gather.4.cloned.1.call-done = bf16[4,80,8192]{2,1,0:T(8,128)(2,1)} async-done(((bf16[1,80,8192]{2,1,0:T(8,128)(2,1)}), bf16[4,80,8192]{2,1,0:T(8,128)(2,1)}) %all-gather.4.cloned.1.call-update) | async-done | bytes 5242896 | tf_op jit(solution)/shard_map/all_gather | solution.py:76
  110.0 0.0 copy-done.2
  110.0 6.1 %fusion.27 = bf16[4,80,256]{2,1,0:T(8,128)(2,1)} fusion(bf16[4,80,8192]{2,1,0:T(8,128)(2,1)} %all-gather.4.cloned.1.call-done, bf16[256,8192]{1,0:T(8,128)(2,1)} %param.17, f32[8192]{0:T(1024)S(1)} %copy-done.2, f32[256]{0:T(256)S(1)} %add_rsqrt_fusion), kind=kOutput, calls=%fused_computation.34 | convolution fusion | flops 1350647808 | bytes 9634816 | tf_op jit(solution)/shard_map/hcd,td->hct/dot_general | solution.py:79
  116.0 3.3 %all-to-all-start = ((bf16[4,80,256]{2,1,0:T(8,128)(2,1)}), bf16[4,80,256]{2,1,0:T(8,128)(2,1)S(1)}, u32[]{:S(2)}, u32[]{:S(2)}) async-start(bf16[4,80,256]{2,1,0:T(8,128)(2,1)} %fusion.27), calls=%async_computation | async-start | bytes 327680 | tf_op jit(solution)/shard_map/all_to_all | solution.py:82
  119.4 0.0 copy-done.1
  119.4 0.0 copy-done
  119.5 11.4 %all-to-all-done = bf16[4,80,256]{2,1,0:T(8,128)(2,1)S(1)} async-done(((bf16[4,80,256]{2,1,0:T(8,128)(2,1)}), bf16[4,80,256]{2,1,0:T(8,128)(2,1)S(1)}, u32[]{:S(2)}, u32[]{:S(2)}) %all-to-all-start) | async-done | bytes 163872 | tf_op jit(solution)/shard_map/all_to_all | solution.py:82
  130.9 4.6 %all_gather.13 = bf16[2,16,1024]{2,1,0:T(8,128)(2,1)S(1)} all-gather(bf16[1,16,1024]{2,1,0:T(8,128)(2,1)S(1)} %slice.30), channel_id=1, replica_groups=mesh['groups'=2,'seq'=4,'fsdp'=2,'sub'=2] {'fsdp'}, dimensions={0}, use_global_device_ids=true | all-gather | bytes 98304 | tf_op jit(solution)/shard_map/all_gather | solution.py:85
  135.5 0.8 gather_fusion
  136.3 0.8 gather_fusion.1
  137.1 0.8 gather_fusion.2
  137.9 0.8 gather_fusion.3
  138.7 0.1 multiply_convert_fusion.3
  138.9 0.1 reshape_squeeze.3
  139.0 0.1 multiply_convert_fusion.2
  139.2 0.3 fusion.34
  139.5 3.5 %while.11 = (s32[]{:T(128)}, f32[2,64,512]{2,1,0:T(8,128)S(1)}, s32[2]{0:T(128)S(1)}, bf16[64,1024]{1,0:T(8,128)(2,1)S(1)}, bf16[16,1024]{1,0:T(8,128)(2,1)S(1)}...) while((s32[]{:T(128)}, f32[2,64,512]{2,1,0:T(8,128)S(1)}, ...), condition=%wide.region_2.3_spmd.clone, body=%wide.region_1.0_spmd.clone.sunk | while | flops 44040196 | bytes 231075 | solution.py:64
  139.5 0.6 dynamic_slice.32
  140.7 0.5 fusion.70
  141.2 0.6 dynamic_slice.32
  142.5 0.5 fusion.70
  142.9 0.3 fusion.31
  143.2 0.2 copy.83
  143.4 0.1 reshape.135
  143.6 0.0 copy-start.3
  143.6 0.5 broadcast.135
  144.1 2.3 %reduce.7 = bf16[1024,64]{1,0:T(8,128)(2,1)S(1)} reduce(bf16[1024,1,64]{2,1,0:T(2,128)(2,1)S(1)} %bitcast.63, bf16[]{:T(256)} %broadcast.135), dimensions={1}, to_apply=%bitcast.51.reduce_sub_computation | reduce | bytes 262146
  146.4 0.2 reshape.137
  146.6 13.8 %all_to_all.33 = bf16[4,2,8192]{2,1,0:T(2,128)(2,1)S(1)} all-to-all(bf16[4,2,8192]{2,1,0:T(2,128)(2,1)S(1)} %reshape.137), channel_id=1, replica_groups=mesh['groups'=2,'seq'=4,'fsdp'=2,'sub'=2] {'seq'}, dimensions={0} | all-to-all | bytes 262144 | tf_op jit(solution)/shard_map/all_to_all | solution.py:92
  160.4 0.3 reshape.138
  160.8 0.3 copy.76
  161.1 0.1 all_to_all.29
  161.2 7.1 %all-gather = bf16[16,1,64,256]{3,2,1,0:T(8,128)(2,1)S(1)} all-gather(bf16[4,1,64,256]{3,2,1,0:T(8,128)(2,1)S(1)} %copy.77), channel_id=2, replica_groups=mesh['groups'=2,'seq'=4,'fsdp'=2,'sub'=2] {'fsdp','sub'}, dimensions={0}, use_global_device_ids=true | all-gather | bytes 655360 | tf_op jit(solution)/shard_map/all_gather | solution.py:93
  168.3 0.1 bitcast_convert_fusion
  168.5 0.1 copy.79
  168.6 0.1 multiply_reduce_fusion
  168.8 28.0 %all-gather.6.cloned.1.call-done = bf16[8,128,2048]{2,1,0:T(8,128)(2,1)} async-done(((bf16[2,128,2048]{2,1,0:T(8,128)(2,1)}), bf16[8,128,2048]{2,1,0:T(8,128)(2,1)}) %all-gather.6.cloned.1.call-update) | async-done | bytes 4194320 | tf_op jit(solution)/shard_map/all_gather | solution.py:77
  196.8 0.0 copy-done.3
  196.8 4.5 %fusion.26 = bf16[256,2048]{1,0:T(8,128)(2,1)} fusion(bf16[8,128,2048]{2,1,0:T(8,128)(2,1)} %all-gather.6.cloned.1.call-done, f32[8,128,256]{2,1,0:T(8,128)S(1)} %bitcast.64, f32[128]{0:T(128)S(1)} %copy-done.3, f32[8,256]{1,0:T(8,128)S(1)} %rsqrt.21), kind=kOutput, calls=%fused_computation.31 | convolution fusion | flops 1075052544 | bytes 6300160 | tf_op jit(solution)/shard_map/het,hed->td/dot_general | solution.py:103
  (27 shorter events, 0.3 us)
Async XLA Ops:
  6.5 103.4 %copy-start.2 = (f32[8192]{0:T(1024)S(1)}, f32[8192]{0:T(1024)}, u32[]{:S(2)}) copy-start(f32[8192]{0:T(1024)} %param.18) | copy-start | bytes 98308
  6.5 103.4 %all-gather.4.cloned.1.call-start = ((), (), s32[]{:S(2)}) async-start(), calls=%async_computation.2 | async-start | bytes 6553600 | tf_op jit(solution)/shard_map/all_gather | solution.py:76
  9.0 187.8 %all-gather.6.cloned.1.call-start = ((), (), s32[]{:S(2)}) async-start(), calls=%async_computation.3 | async-start | bytes 5242880 | tf_op jit(solution)/shard_map/all_gather | solution.py:77
  12.9 106.5 %copy-start.1 = (s32[120]{0:T(128)S(1)}, s32[120]{0:T(128)}, u32[]{:S(2)}) copy-start(s32[120]{0:T(128)} %constant.78) | copy-start | bytes 1444
  12.9 106.5 %copy-start = (s32[120]{0:T(128)S(1)}, s32[120]{0:T(128)}, u32[]{:S(2)}) copy-start(s32[120]{0:T(128)} %constant.79) | copy-start | bytes 1444
  116.0 14.8 %all-to-all-start = ((bf16[4,80,256]{2,1,0:T(8,128)(2,1)}), bf16[4,80,256]{2,1,0:T(8,128)(2,1)S(1)}, u32[]{:S(2)}, u32[]{:S(2)}) async-start(bf16[4,80,256]{2,1,0:T(8,128)(2,1)} %fusion.27), calls=%async_computation | async-start | bytes 327680 | tf_op jit(solution)/shard_map/all_to_all | solution.py:82
  143.6 53.3 %copy-start.3 = (f32[128]{0:T(128)S(1)}, f32[128]{0:T(128)}, u32[]{:S(2)}) copy-start(f32[128]{0:T(128)} %param.22) | copy-start | bytes 1540
Sparse Core Ops, SparseCore 0:
  9.2 100.7 all-gather.3
  111.5 85.2 all-gather.5
where the time goes:
time: 209 us; the launch traced here: 208 us
  waiting for transfers between devices  137 us (66%)
  blocking collectives  25.6 us (12%)
  between operations  13.8 us (7%)
  matrix products  12.1 us (6%)
  other arithmetic  8.29 us (4%)
  local copies, waits for them, and re-layouts  6.51 us (3%)
  starting transfers between devices  3.39 us (2%)
    all_gather x1, waiting for transfers between devices, per_device(): lax.all_gather(stacked, 'seq', axis=0, tiled=True)  97 us
    all_gather x1, waiting for transfers between devices, per_device(): lax.all_gather(w_out, 'seq', axis=0, tiled=True)  28 us
    all_to_all x1, blocking collectives, per_device(): lax.all_to_all(numerator[None], 'seq', split_axis=2, concat_axis=0, tiled...  13.8 us
    all_to_all x1, waiting for transfers between devices, per_device(): lax.all_to_all(projected, 'seq', split_axis=0, concat_axis=2, tiled=True)  11.4 us
    all_gather x1, blocking collectives, per_device(): lax.all_gather(by_token[None], ('fsdp', 'sub'), axis=0, tiled=True)  7.15 us
    dot_general x1, matrix products, per_device(): jnp.einsum('hcd,td->hct', head_weights, normed, preferred_element_type=jn...  6.07 us
    all_gather x1, blocking collectives, per_device(): qk_whole = lax.all_gather(qk_local, 'fsdp', axis=0, tiled=True)  4.58 us
    dot_general x1, matrix products, per_device(): jnp.einsum('het,hed->td', attended, out_weights, preferred_element_type=j...  4.52 us
  transfers between devices with their start and end apart: 3, of which 3 were waited for; matrix products, arithmetic and copies ran while one was open for 10% of the time, Pallas kernels for 0%

commit v1 on v0

--- a/solution.py
+++ b/solution.py
@@ -89,7 +89,10 @@
     numerator = attend(queries, key_vectors, values_local)
     heads_total = out_weights.shape[0]
     head_width = out_weights.shape[1]
-    by_token = lax.all_to_all(numerator[None], "seq", split_axis=2, concat_axis=0, tiled=True)
+    x = numerator[None]
+    cells = jnp.split(x, lax.axis_size("seq"), axis=2)
+    received = lax.all_to_all(jnp.stack(cells), "seq", 0, 0)
+    by_token = jnp.concatenate(received, axis=0)
     everyone = lax.all_gather(by_token[None], ("fsdp", "sub"), axis=0, tiled=True)
     arranged = everyone.reshape(
         lax.axis_size("fsdp"),

time: 209 us -> 209 us (level)
  waiting for transfers between devices: 137 us -> 140 us
  other arithmetic: 8.29 us -> 6.04 us
    all_gather x1, waiting for transfers between devices: 28 us -> 30.6 us  [per_device(): lax.all_gather(w_out, 'seq', axis=0, tiled=True)]
    unnamed x1 -> x0, other arithmetic: 2.27 us -> none
  transfers between devices with their start and end apart: 3 -> 3, of which waited for: 3 -> 3; matrix products, arithmetic and copies ran while one was open for 10% -> 8% of each run, Pallas kernels for 0% -> 0%
where the time goes in v1:
time: 209 us; the launch traced here: 208 us
  waiting for transfers between devices  140 us (67%)
  blocking collectives  26.9 us (13%)
  between operations  13.7 us (7%)
  matrix products  12.1 us (6%)
  other arithmetic  6.04 us (3%)
  local copies, waits for them, and re-layouts  4.94 us (2%)
  starting transfers between devices  3.39 us (2%)
    all_gather x1, waiting for transfers between devices, per_device(): lax.all_gather(stacked, 'seq', axis=0, tiled=True)  97 us
    all_gather x1, waiting for transfers between devices, per_device(): lax.all_gather(w_out, 'seq', axis=0, tiled=True)  30.6 us
    all_to_all x1, blocking collectives, per_device(): received = lax.all_to_all(jnp.stack(cells), 'seq', 0, 0)  15.1 us
    all_to_all x1, waiting for transfers between devices, per_device(): lax.all_to_all(projected, 'seq', split_axis=0, concat_axis=2, tiled=True)  11.4 us
    all_gather x1, blocking collectives, per_device(): lax.all_gather(by_token[None], ('fsdp', 'sub'), axis=0, tiled=True)  7.19 us
    dot_general x1, matrix products, per_device(): jnp.einsum('hcd,td->hct', head_weights, normed, preferred_element_type=jn...  6.07 us
    all_gather x1, blocking collectives, per_device(): qk_whole = lax.all_gather(qk_local, 'fsdp', axis=0, tiled=True)  4.58 us
    dot_general x1, matrix products, per_device(): jnp.einsum('het,hed->td', attended, out_weights, preferred_element_type=j...  4.52 us
  transfers between devices with their start and end apart: 3, of which 3 were waited for; matrix products, arithmetic and copies ran while one was open for 8% of the time, Pallas kernels for 0%

profile of v1, /device:TPU:0, one launch (start us, length us, event | category | flops | bytes accessed | tf_op | source)
XLA Modules:
  0.0 208.2 jit_solution(15778652284450286756)
XLA Ops:
  6.5 0.0 copy-start.2
  6.5 0.0 all-gather.4.cloned.1.call-start
  6.5 2.5 %pad_maximum_fusion = bf16[1,80,8192]{2,1,0:T(8,128)(2,1)} fusion(bf16[1,64,8192]{2,1,0:T(8,128)(2,1)} %param.21, bf16[1,8,8192]{2,1,0:T(8,128)(2,1)} %param.20, bf16[1,8,8192]{2,1,0:T(8,128)(2,1)} %param.19), kind=kLoop, calls=%fused_computation.32 | loop fusion | flops 3932160 | bytes 2621440 | tf_op jit(solution)/shard_map/concatenate | solution.py:74
  9.0 0.0 all-gather.4.cloned.1.call-update
  9.0 0.0 all-gather.6.cloned.1.call-start
  9.1 0.7 all-gather.6.cloned.1.call-update
  9.8 3.1 %fusion.18 = f32[256]{0:T(256)S(1)} fusion(bf16[256,8192]{1,0:T(8,128)(2,1)} %param.17), kind=kLoop, calls=%fused_computation.23 | loop fusion | flops 6291200 | bytes 4195328 | tf_op jit(solution)/shard_map/reduce_sum | solution.py:72
  12.9 0.0 copy-start.1
  12.9 0.0 copy-start
  12.9 97.0 %all-gather.4.cloned.1.call-done = bf16[4,80,8192]{2,1,0:T(8,128)(2,1)} async-done(((bf16[1,80,8192]{2,1,0:T(8,128)(2,1)}), bf16[4,80,8192]{2,1,0:T(8,128)(2,1)}) %all-gather.4.cloned.1.call-update) | async-done | bytes 5242896 | tf_op jit(solution)/shard_map/all_gather | solution.py:76
  110.0 0.0 copy-done.2
  110.0 6.1 %fusion.27 = bf16[4,80,256]{2,1,0:T(8,128)(2,1)} fusion(bf16[4,80,8192]{2,1,0:T(8,128)(2,1)} %all-gather.4.cloned.1.call-done, bf16[256,8192]{1,0:T(8,128)(2,1)} %param.17, f32[8192]{0:T(1024)S(1)} %copy-done.2, f32[256]{0:T(256)S(1)} %add_rsqrt_fusion), kind=kOutput, calls=%fused_computation.34 | convolution fusion | flops 1350647808 | bytes 9634816 | tf_op jit(solution)/shard_map/hcd,td->hct/dot_general | solution.py:79
  116.0 3.3 %all-to-all-start = ((bf16[4,80,256]{2,1,0:T(8,128)(2,1)}), bf16[4,80,256]{2,1,0:T(8,128)(2,1)S(1)}, u32[]{:S(2)}, u32[]{:S(2)}) async-start(bf16[4,80,256]{2,1,0:T(8,128)(2,1)} %fusion.27), calls=%async_computation | async-start | bytes 327680 | tf_op jit(solution)/shard_map/all_to_all | solution.py:82
  119.4 0.0 copy-done.1
  119.4 0.0 copy-done
  119.5 11.4 %all-to-all-done = bf16[4,80,256]{2,1,0:T(8,128)(2,1)S(1)} async-done(((bf16[4,80,256]{2,1,0:T(8,128)(2,1)}), bf16[4,80,256]{2,1,0:T(8,128)(2,1)S(1)}, u32[]{:S(2)}, u32[]{:S(2)}) %all-to-all-start) | async-done | bytes 163872 | tf_op jit(solution)/shard_map/all_to_all | solution.py:82
  130.9 4.6 %all_gather.13 = bf16[2,16,1024]{2,1,0:T(8,128)(2,1)S(1)} all-gather(bf16[1,16,1024]{2,1,0:T(8,128)(2,1)S(1)} %slice.30), channel_id=1, replica_groups=mesh['groups'=2,'seq'=4,'fsdp'=2,'sub'=2] {'fsdp'}, dimensions={0}, use_global_device_ids=true | all-gather | bytes 98304 | tf_op jit(solution)/shard_map/all_gather | solution.py:85
  135.5 0.8 gather_fusion
  136.3 0.8 gather_fusion.1
  137.1 0.8 gather_fusion.2
  137.9 0.8 gather_fusion.3
  138.7 0.1 multiply_convert_fusion.3
  138.9 0.1 reshape_squeeze.3
  139.0 0.1 multiply_convert_fusion.2
  139.2 0.3 fusion.34
  139.5 3.5 %while.11 = (s32[]{:T(128)}, f32[2,64,512]{2,1,0:T(8,128)S(1)}, s32[2]{0:T(128)S(1)}, bf16[64,1024]{1,0:T(8,128)(2,1)S(1)}, bf16[16,1024]{1,0:T(8,128)(2,1)S(1)}...) while((s32[]{:T(128)}, f32[2,64,512]{2,1,0:T(8,128)S(1)}, ...), condition=%wide.region_2.3_spmd.clone, body=%wide.region_1.0_spmd.clone.sunk | while | flops 44040196 | bytes 231075 | solution.py:64
  139.5 0.6 dynamic_slice.32
  140.7 0.5 fusion.70
  141.2 0.6 dynamic_slice.32
  142.5 0.5 fusion.70
  142.9 0.0 copy-start.3
  143.0 0.3 fusion.31
  143.2 0.1 copy.65
  143.4 0.1 broadcast_in_dim_reshape.6
  143.5 15.1 %all_to_all.23 = bf16[4,1,64,256]{3,2,1,0:T(8,128)(2,1)S(1)} all-to-all(bf16[4,1,64,256]{3,2,1,0:T(8,128)(2,1)S(1)} %pad_maximum_fusion.1), channel_id=1, replica_groups=mesh['groups'=2,'seq'=4,'fsdp'=2,'sub'=2] {'seq'}, dimensions={0} | all-to-all | bytes 262144 | tf_op jit(solution)/shard_map/all_to_all | solution.py:94
  158.6 7.2 %all-gather = bf16[16,1,64,256]{3,2,1,0:T(8,128)(2,1)S(1)} all-gather(bf16[4,1,64,256]{3,2,1,0:T(8,128)(2,1)S(1)} %all_to_all.23), channel_id=2, replica_groups=mesh['groups'=2,'seq'=4,'fsdp'=2,'sub'=2] {'fsdp','sub'}, dimensions={0}, use_global_device_ids=true | all-gather | bytes 655360 | tf_op jit(solution)/shard_map/all_gather | solution.py:96
  165.8 0.1 bitcast_convert_fusion
  165.9 0.1 copy.67
  166.0 0.1 multiply_reduce_fusion
  166.3 30.6 %all-gather.6.cloned.1.call-done = bf16[8,128,2048]{2,1,0:T(8,128)(2,1)} async-done(((bf16[2,128,2048]{2,1,0:T(8,128)(2,1)}), bf16[8,128,2048]{2,1,0:T(8,128)(2,1)}) %all-gather.6.cloned.1.call-update) | async-done | bytes 4194320 | tf_op jit(solution)/shard_map/all_gather | solution.py:77
  196.8 0.0 copy-done.3
  196.8 4.5 %fusion.26 = bf16[256,2048]{1,0:T(8,128)(2,1)} fusion(bf16[8,128,2048]{2,1,0:T(8,128)(2,1)} %all-gather.6.cloned.1.call-done, f32[8,128,256]{2,1,0:T(8,128)S(1)} %bitcast.65, f32[128]{0:T(128)S(1)} %copy-done.3, f32[8,256]{1,0:T(8,128)S(1)} %rsqrt.21), kind=kOutput, calls=%fused_computation.31 | convolution fusion | flops 1075052544 | bytes 6300160 | tf_op jit(solution)/shard_map/het,hed->td/dot_general | solution.py:106
  (28 shorter events, 0.3 us)
Async XLA Ops:
  6.5 103.4 %copy-start.2 = (f32[8192]{0:T(1024)S(1)}, f32[8192]{0:T(1024)}, u32[]{:S(2)}) copy-start(f32[8192]{0:T(1024)} %param.18) | copy-start | bytes 98308
  6.5 103.4 %all-gather.4.cloned.1.call-start = ((), (), s32[]{:S(2)}) async-start(), calls=%async_computation.2 | async-start | bytes 6553600 | tf_op jit(solution)/shard_map/all_gather | solution.py:76
  9.0 187.8 %all-gather.6.cloned.1.call-start = ((), (), s32[]{:S(2)}) async-start(), calls=%async_computation.3 | async-start | bytes 5242880 | tf_op jit(solution)/shard_map/all_gather | solution.py:77
  12.9 106.5 %copy-start.1 = (s32[120]{0:T(128)S(1)}, s32[120]{0:T(128)}, u32[]{:S(2)}) copy-start(s32[120]{0:T(128)} %constant.78) | copy-start | bytes 1444
  12.9 106.5 %copy-start = (s32[120]{0:T(128)S(1)}, s32[120]{0:T(128)}, u32[]{:S(2)}) copy-start(s32[120]{0:T(128)} %constant.79) | copy-start | bytes 1444
  116.0 14.8 %all-to-all-start = ((bf16[4,80,256]{2,1,0:T(8,128)(2,1)}), bf16[4,80,256]{2,1,0:T(8,128)(2,1)S(1)}, u32[]{:S(2)}, u32[]{:S(2)}) async-start(bf16[4,80,256]{2,1,0:T(8,128)(2,1)} %fusion.27), calls=%async_computation | async-start | bytes 327680 | tf_op jit(solution)/shard_map/all_to_all | solution.py:82
  142.9 53.9 %copy-start.3 = (f32[128]{0:T(128)S(1)}, f32[128]{0:T(128)}, u32[]{:S(2)}) copy-start(f32[128]{0:T(128)} %param.22) | copy-start | bytes 1540
Sparse Core Ops, SparseCore 0:
  9.2 100.7 all-gather.3
  111.5 85.2 all-gather.5
